TPU v7x, 512 devices: a whole 4x4x16 slice. The times are simulated.
512 devices in a mesh: row: 32 (over z, core), col: 16 (over x, y).
Axes of the slice: x: 4, y: 4, z: 16, core: 2. Of those that a mesh axis runs over, the one named last changes fastest.
Arguments:
- factor: bfloat16 [8192, 8192], P('row', 'col'), as said below
- sel_tiles: int32 [32], replicated, may hold values from 0 to 63, as said below
- coupling: bfloat16 [8192, 2048], P('col', 'row')
Outputs:
- root_inverse: float32 [8192, 8192], P('row', 'col')
- child_inverse: float32 [2048, 8192], P('col', 'row')
Inputs may be any that keep to these rules, and one draw needn't show every extreme that they name: sel_tiles holds 32 distinct tile indices in increasing order; rows of coupling outside the listed tiles are zero. factor is lower triangular with a diagonal between 1 and 1.5.
All inputs are finite; a program needn't handle non-finite values.
Results may differ from a plain program's by a relative error of at most 0.003.
Values may be sent and summed in bfloat16 or wider, within the bound.
A program may use at most 64 MiB of HBM per device.

v0:
```python
import jax
import jax.numpy as jnp
from jax import lax
from jax.sharding import PartitionSpec as P

TILE = 128


def from_root(value, axis, source):
    kept = jnp.where(lax.axis_index(axis) == source, value, 0).astype(value.dtype)
    return lax.psum(kept, axis)


def in_blocks(value, dim, devices):
    lengths = value.shape
    parts = value.reshape(*lengths[:dim], devices, lengths[dim] // devices, *lengths[dim + 1 :])
    return jnp.moveaxis(parts, dim, 0)


def summed_on_arrival(value, axis, dim):
    devices = lax.axis_size(axis)
    parts = lax.all_to_all(in_blocks(value, dim, devices), axis, 0, 0, tiled=True)
    return jnp.sum(parts, axis=0)


def body(factor, sel_tiles, coupling):
    rows_here = factor.shape[0]
    row_index = lax.axis_index("row")
    whole = lax.all_gather(factor, "row", axis=0, tiled=True)
    ratio = lax.axis_size("row") // lax.axis_size("col")
    offset = row_index % ratio * rows_here
    piece = lax.dynamic_slice_in_dim(whole, offset, rows_here, 1)
    partner = from_root(piece, "col", row_index // ratio)
    gram = lax.dot_general(
        partner, whole, (((0,), (0,)), ((), ())), preferred_element_type=jnp.float32
    )
    coupling_full = lax.all_gather(coupling, "row", axis=1, tiled=True)
    rounded = gram.astype(jnp.bfloat16)
    global_rows = row_index * rows_here + jnp.arange(rows_here, dtype=jnp.int32)
    member = jnp.any((global_rows // TILE)[:, None] == sel_tiles[None, :], axis=1)
    summed = summed_on_arrival(
        lax.dot_general(
            coupling_full, rounded, (((0,), (1,)), ((), ())), preferred_element_type=jnp.float32
        ),
        "col",
        0,
    )
    child = jnp.where(member[None, :], -summed, jnp.float32(0.0))
    return (gram, child)


def solution(mesh):
    placed = (P("row", "col"), P(), P("col", "row"))
    return jax.shard_map(
        body,
        mesh=mesh,
        in_specs=placed,
        out_specs=(P("row", "col"), P("col", "row")),
        check_vma=False,
    )
```

profile of v0, /device:TPU:32, one launch (start us, length us, event | category | flops | bytes accessed | tf_op | source)
XLA Modules:
  0.0 351.7 jit_solution(12061191900237767093)
XLA Ops:
  7.2 0.0 all-gather.3.cloned.1.call-start
  7.2 0.7 all-gather.3.cloned.1.call-update
  7.9 0.0 all-reduce.2.cloned.1.call-start
  8.0 84.9 %all-gather.3.cloned.1.call-done = bf16[8192,512]{1,0:T(8,128)(2,1)} async-done(((bf16[256,512]{1,0:T(8,128)(2,1)}), bf16[8192,512]{1,0:T(8,128)(2,1)}) %all-gather.3.cloned.1.call-update) | async-done | bytes 8388624 | tf_op jit(solution)/shard_map/all_gather | solution.py:29
  92.8 4.9 %dynamic-slice_select_fusion = bf16[8192,256]{1,0:T(8,128)(2,1)} fusion(bf16[8192,512]{1,0:T(8,128)(2,1)} %all-gather.3.cloned.1.call-done, s32[]{:T(128)S(6)} %select_n.38, pred[]{:T(512)S(6)} %eq.18), kind=kLoop, calls=%fused_computation | loop fusion | flops 2097152 | bytes 8388613 | tf_op jit(solution)/shard_map/jit(_where)/select_n | solution.py:10
  97.7 0.0 all-reduce.2.cloned.1.call-update
  97.7 0.0 all-gather.5.cloned.1.call-start
  97.8 0.7 all-gather.5.cloned.1.call-update
  98.5 130.4 %all-reduce.2.cloned.1.call-done = bf16[8192,256]{1,0:T(8,128)(2,1)} async-done(((bf16[8192,256]{1,0:T(8,128)(2,1)}), bf16[8192,256]{1,0:T(8,128)(2,1)}) %all-reduce.2.cloned.1.call-update) | async-done | bytes 4194320 | tf_op jit(solution)/shard_map/psum | solution.py:11
  228.9 7.0 %fusion.1 = f32[256,512]{1,0:T(8,128)S(1)} fusion(bf16[8192,256]{1,0:T(8,128)(2,1)} %all-reduce.2.cloned.1.call-done, bf16[8192,512]{1,0:T(8,128)(2,1)} %all-gather.3.cloned.1.call-done), kind=kOutput, calls=%fused_computation.10 | convolution fusion | flops 2147483648 | bytes 13107200 | tf_op jit(solution)/shard_map/dot_general | solution.py:34
  235.9 0.0 copy-start
  235.9 66.4 %all-gather.5.cloned.1.call-done = bf16[512,2048]{0,1:T(8,128)(2,1)} async-done(((bf16[512,64]{0,1:T(8,128)(2,1)}), bf16[512,2048]{0,1:T(8,128)(2,1)}) %all-gather.5.cloned.1.call-update) | async-done | bytes 2097168 | tf_op jit(solution)/shard_map/all_gather | solution.py:37
  302.3 2.3 convolution_bitcast_fusion
  304.7 0.0 copy-start.1
  304.7 1.5 copy.14
  306.2 0.0 copy-done
  306.2 6.9 %all-to-all-start = ((f32[16,128,256]{1,2,0:T(8,128)}), f32[16,128,256]{1,2,0:T(8,128)S(1)}, u32[]{:S(2)}, u32[]{:S(2)}) async-start(f32[16,128,256]{1,2,0:T(8,128)} %bitcast.9), calls=%async_computation | async-start | bytes 4194304 | tf_op jit(solution)/shard_map/all_to_all | solution.py:22
  313.1 0.0 copy-done.1
  313.1 0.1 compare_reduce_fusion
  313.2 30.9 %all-to-all-done = f32[16,128,256]{1,2,0:T(8,128)S(1)} async-done(((f32[16,128,256]{1,2,0:T(8,128)}), f32[16,128,256]{1,2,0:T(8,128)S(1)}, u32[]{:S(2)}, u32[]{:S(2)}) %all-to-all-start) | async-done | bytes 2097184 | tf_op jit(solution)/shard_map/all_to_all | solution.py:22
  344.2 0.1 reduce_sum.9
  344.3 0.1 negate_select_fusion
  344.4 0.8 copy.10
  (1 shorter events, 0.0 us)
Async XLA Ops:
  7.2 85.7 %all-gather.3.cloned.1.call-start = ((), (), s32[]{:S(2)}) async-start(), calls=%async_computation.1 | async-start | bytes 8650752 | tf_op jit(solution)/shard_map/all_gather | solution.py:29
  7.9 221.0 %all-reduce.2.cloned.1.call-start = ((), (), s32[]{:S(2)}) async-start(), calls=%async_computation.2 | async-start | bytes 8388608 | tf_op jit(solution)/shard_map/psum | solution.py:11
  97.7 204.6 %all-gather.5.cloned.1.call-start = ((), (), s32[]{:S(2)}) async-start(), calls=%async_computation.3 | async-start | bytes 2162688 | tf_op jit(solution)/shard_map/all_gather | solution.py:37
  235.9 70.3 %copy-start = (f32[256,512]{1,0:T(8,128)}, f32[256,512]{1,0:T(8,128)S(1)}, u32[]{:S(2)}) copy-start(f32[256,512]{1,0:T(8,128)S(1)} %fusion.1) | copy-start | bytes 1572868
  304.7 8.5 %copy-start.1 = (s32[32]{0:T(128)S(1)}, s32[32]{0:T(128)}, u32[]{:S(2)}) copy-start(s32[32]{0:T(128)} %param.4) | copy-start | bytes 388
  306.2 37.9 %all-to-all-start = ((f32[16,128,256]{1,2,0:T(8,128)}), f32[16,128,256]{1,2,0:T(8,128)S(1)}, u32[]{:S(2)}, u32[]{:S(2)}) async-start(f32[16,128,256]{1,2,0:T(8,128)} %bitcast.9), calls=%async_computation | async-start | bytes 4194304 | tf_op jit(solution)/shard_map/all_to_all | solution.py:22
Sparse Core Ops, SparseCore 0:
  10.1 82.6 all-gather.2
  97.8 130.9 all-reduce.1
  231.0 71.2 all-gather.4
where the time goes:
time: 352 us
  waiting for transfers between devices  314 us (89%)
  between operations  13.8 us (4%)
  matrix products  9.32 us (3%)
  starting transfers between devices  7.01 us (2%)
  other arithmetic  5.17 us (1%)
    psum x1, waiting for transfers between devices, from_root(): return lax.psum(kept, axis)  130 us
    all_gather x1, waiting for transfers between devices, body(): whole = lax.all_gather(factor, 'row', axis=0, tiled=True)  84.9 us
    all_gather x1, waiting for transfers between devices, body(): coupling_full = lax.all_gather(coupling, 'row', axis=1, tiled=True)  66.4 us
    all_to_all x1, waiting for transfers between devices, summed_on_arrival(): lax.all_to_all(in_blocks(value, dim, devices), axis, 0, 0, tiled=True)  30.9 us
  transfers between devices with their start and end apart: 4, of which 4 were waited for; matrix products, arithmetic and copies ran while one was open for 2% of the time, Pallas kernels for 0%

commit v1 on v0

--- a/solution.py
+++ b/solution.py
@@ -26,7 +26,9 @@
 def body(factor, sel_tiles, coupling):
     rows_here = factor.shape[0]
     row_index = lax.axis_index("row")
-    whole = lax.all_gather(factor, "row", axis=0, tiled=True)
+    whole = jnp.concatenate(
+        lax.all_to_all(jnp.stack([factor] * lax.axis_size("row")), "row", 0, 0), axis=0
+    )
     ratio = lax.axis_size("row") // lax.axis_size("col")
     offset = row_index % ratio * rows_here
     piece = lax.dynamic_slice_in_dim(whole, offset, rows_here, 1)

time: 352 us -> 585 us (1.66)
  waiting for transfers between devices: 314 us -> 526 us
  starting transfers between devices: 7.01 us -> 20.8 us
    all_to_all x0 -> x1, waiting for transfers between devices: none -> 370 us  [body(): lax.all_to_all(jnp.stack([factor] * lax.axis_size('row')), 'row', 0, 0)]
    all_gather x1 -> x0, waiting for transfers between devices: 84.9 us -> none  [body(): whole = lax.all_gather(factor, 'row', axis=0, tiled=True)]
    all_gather x1, waiting for transfers between devices: 66.4 us -> 0.03 us  [body(): coupling_full = lax.all_gather(coupling, 'row', axis=1, tiled=True)]
    all_to_all x0 -> x1, starting transfers between devices: none -> 15.4 us  [body(): lax.all_to_all(jnp.stack([factor] * lax.axis_size('row')), 'row', 0, 0)]
  transfers between devices with their start and end apart: 4 -> 4, of which waited for: 4 -> 3; matrix products, arithmetic and copies ran while one was open for 2% -> 1% of each run, Pallas kernels for 0% -> 0%
where the time goes in v1:
time: 585 us
  waiting for transfers between devices  526 us (90%)
  starting transfers between devices  20.8 us (4%)
  between operations  15.6 us (3%)
  matrix products  9.48 us (2%)
  local copies, waits for them, and re-layouts  7.43 us (1%)
    all_to_all x1, waiting for transfers between devices, body(): lax.all_to_all(jnp.stack([factor] * lax.axis_size('row')), 'row', 0, 0)  370 us
    psum x1, waiting for transfers between devices, from_root(): return lax.psum(kept, axis)  126 us
    all_to_all x1, waiting for transfers between devices, summed_on_arrival(): lax.all_to_all(in_blocks(value, dim, devices), axis, 0, 0, tiled=True)  30 us
    all_to_all x1, starting transfers between devices, body(): lax.all_to_all(jnp.stack([factor] * lax.axis_size('row')), 'row', 0, 0)  15.4 us
  transfers between devices with their start and end apart: 4, of which 3 were waited for; matrix products, arithmetic and copies ran while one was open for 1% of the time, Pallas kernels for 0%

profile of v1, /device:TPU:32, one launch (start us, length us, event | category | flops | bytes accessed | tf_op | source)
XLA Modules:
  0.0 584.9 jit_solution(17080301382215973626)
XLA Ops:
  8.0 5.1 stack.2
  13.1 15.4 %all-to-all-start = ((bf16[32,256,512]{2,1,0:T(8,128)(2,1)}), bf16[32,256,512]{2,1,0:T(8,128)(2,1)}, u32[]{:S(2)}, u32[]{:S(2)}) async-start(bf16[32,256,512]{2,1,0:T(8,128)(2,1)} %stack.2), calls=%async_computation | async-start | bytes 16777216 | tf_op jit(solution)/shard_map/all_to_all | solution.py:30
  28.5 0.0 all-reduce.2.cloned.1.call-start
  28.6 369.9 %all-to-all-done = bf16[32,256,512]{2,1,0:T(8,128)(2,1)} async-done(((bf16[32,256,512]{2,1,0:T(8,128)(2,1)}), bf16[32,256,512]{2,1,0:T(8,128)(2,1)}, u32[]{:S(2)}, u32[]{:S(2)}) %all-to-all-start) | async-done | bytes 8388640 | tf_op jit(solution)/shard_map/all_to_all | solution.py:30
  398.5 4.9 dynamic-slice_select_fusion
  403.3 0.0 all-reduce.2.cloned.1.call-update
  403.3 0.0 all-gather.2.cloned.1.call-start
  403.4 0.5 all-gather.2.cloned.1.call-update
  403.9 126.1 %all-reduce.2.cloned.1.call-done = bf16[8192,256]{1,0:T(8,128)(2,1)} async-done(((bf16[8192,256]{1,0:T(8,128)(2,1)}), bf16[8192,256]{1,0:T(8,128)(2,1)}) %all-reduce.2.cloned.1.call-update) | async-done | bytes 4194320 | tf_op jit(solution)/shard_map/psum | solution.py:11
  530.0 7.0 %fusion.1 = f32[256,512]{1,0:T(8,128)S(1)} fusion(bf16[8192,256]{1,0:T(8,128)(2,1)} %all-reduce.2.cloned.1.call-done, bf16[8192,512]{1,0:T(8,128)(2,1)} %bitcast), kind=kOutput, calls=%fused_computation.10 | convolution fusion | flops 2147483648 | bytes 13107200 | tf_op jit(solution)/shard_map/dot_general | solution.py:36
  537.0 0.0 copy-start
  537.0 0.0 all-gather.2.cloned.1.call-done
  537.0 2.5 convolution_bitcast_fusion
  539.5 0.0 copy-start.1
  539.6 1.5 copy.14
  541.1 0.0 copy-done
  541.1 5.3 all-to-all-start.1
  546.5 0.0 copy-done.1
  546.5 0.1 compare_reduce_fusion
  546.6 30.0 %all-to-all-done.1 = f32[16,128,256]{1,2,0:T(8,128)S(1)} async-done(((f32[16,128,256]{1,2,0:T(8,128)}), f32[16,128,256]{1,2,0:T(8,128)S(1)}, u32[]{:S(2)}, u32[]{:S(2)}) %all-to-all-start.1) | async-done | bytes 2097184 | tf_op jit(solution)/shard_map/all_to_all | solution.py:22
  576.5 0.1 reduce_sum.9
  576.6 0.1 negate_select_fusion
  576.7 0.8 copy.10
  (1 shorter events, 0.0 us)
Async XLA Ops:
  13.1 385.3 %all-to-all-start = ((bf16[32,256,512]{2,1,0:T(8,128)(2,1)}), bf16[32,256,512]{2,1,0:T(8,128)(2,1)}, u32[]{:S(2)}, u32[]{:S(2)}) async-start(bf16[32,256,512]{2,1,0:T(8,128)(2,1)} %stack.2), calls=%async_computation | async-start | bytes 16777216 | tf_op jit(solution)/shard_map/all_to_all | solution.py:30
  28.5 501.5 %all-reduce.2.cloned.1.call-start = ((), (), s32[]{:S(2)}) async-start(), calls=%async_computation.2 | async-start | bytes 8388608 | tf_op jit(solution)/shard_map/psum | solution.py:11
  403.3 133.7 %all-gather.2.cloned.1.call-start = ((), (), s32[]{:S(2)}) async-start(), calls=%async_computation.3 | async-start | bytes 2162688 | tf_op jit(solution)/shard_map/all_gather | solution.py:39
  537.0 4.1 copy-start
  539.5 6.9 %copy-start.1 = (s32[32]{0:T(128)S(1)}, s32[32]{0:T(128)}, u32[]{:S(2)}) copy-start(s32[32]{0:T(128)} %param.4) | copy-start | bytes 388
  541.1 35.4 %all-to-all-start.1 = ((f32[16,128,256]{1,2,0:T(8,128)}), f32[16,128,256]{1,2,0:T(8,128)S(1)}, u32[]{:S(2)}, u32[]{:S(2)}) async-start(f32[16,128,256]{1,2,0:T(8,128)} %bitcast.10), calls=%async_computation.1 | async-start | bytes 4194304 | tf_op jit(solution)/shard_map/all_to_all | solution.py:22
Sparse Core Ops, SparseCore 0:
  403.5 126.4 all-reduce.1
Sparse Core Ops, SparseCore 1:
  406.0 63.6 all-gather.1
